TPU v7x, 32 devices: a whole 2x2x4 slice. The times are simulated.
32 devices in a mesh: dp: 8 (over y, x, core), tensor: 4 (over z).
Axes of the slice: x: 2, y: 2, z: 4, core: 2. Of those that a mesh axis runs over, the one named last changes fastest.
Arguments:
- block_in: bfloat16 [16384, 2048], P(('dp', 'tensor')), may hold values from -6 to 6
- ln_gain: float32 [2048], replicated, may hold values from 0.5 to 1.5
- ln_bias: float32 [2048], replicated, may hold values from -3 to 3
- qkv_weight: bfloat16 [3, 2048, 2048], P(None, None, 'tensor'), may hold values from -1 to 1
- qkv_bias: float32 [3, 2048], P(None, 'tensor'), may hold values from -3 to 3
- out_weight: bfloat16 [2048, 2048], P('tensor'), may hold values from -0.5 to 0.5
- out_bias: float32 [2048], replicated, may hold values from -3 to 3
- up_weight: bfloat16 [2048, 8192], P(None, 'tensor'), may hold values from -0.125 to 0.125
- up_bias: float32 [8192], P('tensor'), may hold values from -3 to 3
- down_weight: bfloat16 [8192, 2048], P('tensor'), may hold values from -0.0625 to 0.0625
- down_bias: float32 [2048], replicated, may hold values from -3 to 3
- segments: int32 [16384], P('dp'), may hold values from 0 to 3, as said below
- cotangent: bfloat16 [16384, 2048], P(('dp', 'tensor')), may hold values from -6 to 6
Outputs:
- block_out: bfloat16 [16384, 2048], P(('dp', 'tensor'))
- input_grad: bfloat16 [16384, 2048], P(('dp', 'tensor'))
- ln_gain_grad: float32 [2048], replicated
- ln_bias_grad: float32 [2048], replicated
- qkv_weight_grad: float32 [3, 2048, 2048], P(None, 'dp', 'tensor')
- qkv_bias_grad: float32 [3, 2048], P(None, 'tensor')
- out_weight_grad: float32 [2048, 2048], P('tensor', 'dp')
- out_bias_grad: float32 [2048], replicated
- up_weight_grad: float32 [2048, 8192], P('dp', 'tensor')
- up_bias_grad: float32 [8192], P('tensor')
- down_weight_grad: float32 [8192, 2048], P('tensor', 'dp')
- down_bias_grad: float32 [2048], replicated
Inputs may be any that keep to these rules, and one draw needn't show every extreme that they name: `segments`: along each sequence of 2048 tokens the segment numbers start at 0, never fall, and rise by one at each of three document starts.
All inputs are finite; a program needn't handle non-finite values.
Results may differ from a plain program's by a relative error of at most 0.012.
Values may be sent and summed in bfloat16 or wider, within the bound.
A program may use at most 320 MiB of HBM per device.

v0:
```python
import jax
import jax.numpy as jnp
from jax import lax
from jax.sharding import PartitionSpec as P

D = 2048
HD = 64
ROT = 32
FF = 8192


EPSILON = 1e-05
NEGATIVE = -1e30
ROOT_TWO_PI = 0.7978845608028654


def normalize(rows):
    wide = rows.astype(jnp.float32)
    centre = wide - jnp.mean(wide, axis=-1, keepdims=True)
    inv_scale = lax.rsqrt(jnp.mean(centre * centre, axis=-1, keepdims=True) + EPSILON)
    return (centre * inv_scale, inv_scale)


def gelu_pair(pre):
    inner = ROOT_TWO_PI * (pre + 0.044715 * pre * pre * pre)
    tangent = jnp.tanh(inner)
    value = 0.5 * pre * (1.0 + tangent)
    slope = 0.5 * (1.0 + tangent) + 0.5 * pre * (1.0 - tangent * tangent) * ROOT_TWO_PI * (
        1.0 + 3.0 * 0.044715 * pre * pre
    )
    return (value, slope)


def rotary_tables(segments, rotary):
    length = segments.shape[0]
    index = jnp.arange(length, dtype=jnp.int32)
    first = jnp.concatenate([jnp.ones((1,), jnp.bool_), segments[1:] != segments[:-1]])
    starts = lax.cummax(jnp.where(first, index, jnp.zeros_like(index)), axis=0)
    place = (index - starts).astype(jnp.float32)
    freq = 10000.0 ** (-(2.0 * jnp.arange(rotary // 2, dtype=jnp.float32)) / rotary)
    angle = place[:, None] * freq[None, :]
    return (jnp.cos(angle), jnp.sin(angle))


def rotate(values, cosine, sine, rotary):
    half = rotary // 2
    first = values[..., :half]
    second = values[..., half:rotary]
    cosine = cosine[:, None, :]
    sine = sine[:, None, :]
    return jnp.concatenate(
        [first * cosine - second * sine, second * cosine + first * sine, values[..., rotary:]],
        axis=-1,
    )


def unrotate(grads, cosine, sine, rotary):
    half = rotary // 2
    first = grads[..., :half]
    second = grads[..., half:rotary]
    cosine = cosine[:, None, :]
    sine = sine[:, None, :]
    return jnp.concatenate(
        [first * cosine + second * sine, second * cosine - first * sine, grads[..., rotary:]],
        axis=-1,
    )


def allowed_block(segments, start, end):
    query_index = jnp.arange(start, end, dtype=jnp.int32)
    key_index = jnp.arange(end, dtype=jnp.int32)
    causal = key_index[None, :] <= query_index[:, None]
    same = segments[None, :end] == segments[start:end, None]
    return causal & same


def block_scores(query, key, segments, start, end):
    scores = jnp.einsum(
        "qhd,khd->hqk", query[start:end], key[:end], preferred_element_type=jnp.float32
    ) * HD ** (-0.5)
    return jnp.where(allowed_block(segments, start, end)[None], scores, NEGATIVE)


def local(
    block_in,
    ln_gain,
    ln_bias,
    qkv_weight,
    qkv_bias,
    out_weight,
    out_bias,
    up_weight,
    up_bias,
    down_weight,
    down_bias,
    segments,
    cotangent,
):
    local_rows = block_in.shape[0]
    cols = qkv_weight.shape[2]
    units = up_weight.shape[1]
    heads = cols // HD
    whole_in = lax.all_gather(block_in, "tensor", axis=0, tiled=True)
    normed_all, scale_all = normalize(whole_in)
    hidden = (normed_all * ln_gain + ln_bias).astype(jnp.bfloat16)
    offset = lax.axis_index("tensor") * local_rows
    normed = lax.dynamic_slice_in_dim(normed_all, offset, local_rows, 0)
    inv_scale = lax.dynamic_slice_in_dim(scale_all, offset, local_rows, 0)
    length = hidden.shape[0]
    cosine, sine = rotary_tables(segments, ROT)
    projected = (
        jnp.einsum("tm,cml->ctl", hidden, qkv_weight, preferred_element_type=jnp.float32)
        + qkv_bias[:, None, :]
    )
    query = rotate(projected[0].reshape(length, heads, HD), cosine, sine, ROT).astype(jnp.bfloat16)
    key = rotate(projected[1].reshape(length, heads, HD), cosine, sine, ROT).astype(jnp.bfloat16)
    value = projected[2].reshape(length, heads, HD).astype(jnp.bfloat16)
    step = min(512, length)
    results = []
    totals = []
    for start in range(0, length, step):
        end = start + step
        scores = block_scores(query, key, segments, start, end)
        peak = jnp.max(scores, axis=-1, keepdims=True)
        total = peak + jnp.log(jnp.sum(jnp.exp(scores - peak), axis=-1, keepdims=True))
        probs = jnp.exp(scores - total).astype(jnp.bfloat16)
        results.append(
            jnp.einsum(
                "hqk,khd->qhd", probs, value[:end], preferred_element_type=jnp.float32
            ).astype(jnp.bfloat16)
        )
        totals.append(total)
    attended = jnp.concatenate(results, axis=0)
    log_sums = jnp.concatenate(totals, axis=1)
    attended_flat = attended.reshape(length, cols)
    act_pre = jnp.dot(hidden, up_weight, preferred_element_type=jnp.float32) + up_bias
    act_value, act_slope = gelu_pair(act_pre)
    act = act_value.astype(jnp.bfloat16)
    rows_act = act
    branch = lax.psum_scatter(
        (
            jnp.dot(attended_flat, out_weight, preferred_element_type=jnp.float32)
            + jnp.dot(rows_act, down_weight, preferred_element_type=jnp.float32)
        ).astype(jnp.bfloat16),
        "tensor",
        scatter_dimension=0,
        tiled=True,
    ).astype(jnp.float32)
    block_out = (block_in.astype(jnp.float32) + branch + out_bias + down_bias).astype(jnp.bfloat16)
    bias_sum = jnp.sum(cotangent.astype(jnp.float32), axis=0)
    grad_out = lax.all_gather(cotangent, "tensor", axis=0, tiled=True)
    contract_rows = (((0,), (0,)), ((), ()))
    contract_cols = (((1,), (1,)), ((), ()))
    down_grad = lax.dot_general(act, grad_out, contract_rows, preferred_element_type=jnp.float32)
    out_grad = lax.dot_general(
        attended_flat, grad_out, contract_rows, preferred_element_type=jnp.float32
    )
    act_grad = (
        lax.dot_general(grad_out, down_weight, contract_cols, preferred_element_type=jnp.float32)
        * act_slope
    )
    up_bias_local = jnp.sum(act_grad, axis=0)
    act_grad_b = act_grad.astype(jnp.bfloat16)
    up_grad = lax.dot_general(hidden, act_grad_b, contract_rows, preferred_element_type=jnp.float32)
    attended_grad = (
        lax.dot_general(grad_out, out_weight, contract_cols, preferred_element_type=jnp.float32)
        .astype(jnp.bfloat16)
        .reshape(length, heads, HD)
    )
    query_parts = []
    key_grad = jnp.zeros((length, heads, HD), jnp.float32)
    value_grad = jnp.zeros((length, heads, HD), jnp.float32)
    for start in range(0, length, step):
        end = start + step
        scores = block_scores(query, key, segments, start, end)
        probs_f = jnp.exp(scores - log_sums[:, start:end])
        probs = probs_f.astype(jnp.bfloat16)
        grad_rows = attended_grad[start:end]
        value_grad = value_grad.at[:end].add(
            jnp.einsum("hqk,qhd->khd", probs, grad_rows, preferred_element_type=jnp.float32)
        )
        probs_grad = jnp.einsum(
            "qhd,khd->hqk", grad_rows, value[:end], preferred_element_type=jnp.float32
        )
        delta = jnp.einsum(
            "qhd,qhd->hq", grad_rows, attended[start:end], preferred_element_type=jnp.float32
        )
        score_grad = (probs_f * (probs_grad - delta[..., None]) * HD ** (-0.5)).astype(jnp.bfloat16)
        query_parts.append(
            jnp.einsum("hqk,khd->qhd", score_grad, key[:end], preferred_element_type=jnp.float32)
        )
        key_grad = key_grad.at[:end].add(
            jnp.einsum(
                "hqk,qhd->khd", score_grad, query[start:end], preferred_element_type=jnp.float32
            )
        )
    query_grad = unrotate(jnp.concatenate(query_parts, axis=0), cosine, sine, ROT).reshape(
        length, cols
    )
    key_grad = unrotate(key_grad, cosine, sine, ROT).reshape(length, cols)
    projected_grad = jnp.stack([query_grad, key_grad, value_grad.reshape(length, cols)])
    qkv_bias_local = jnp.sum(projected_grad, axis=1)
    projected_grad_b = projected_grad.astype(jnp.bfloat16)
    qkv_grad = jnp.einsum(
        "tm,ctl->cml", hidden, projected_grad_b, preferred_element_type=jnp.float32
    )
    rows_act = act_grad_b
    term = jnp.einsum(
        "crl,cml->rm", projected_grad_b, qkv_weight, preferred_element_type=jnp.float32
    )
    hidden_grad = lax.psum_scatter(
        (
            term
            + lax.dot_general(
                rows_act, up_weight, contract_cols, preferred_element_type=jnp.float32
            )
        ).astype(jnp.bfloat16),
        "tensor",
        scatter_dimension=0,
        tiled=True,
    ).astype(jnp.float32)
    gain_local = jnp.sum(hidden_grad * normed, axis=0)
    shift_local = jnp.sum(hidden_grad, axis=0)
    scaled = hidden_grad * ln_gain
    inner = (
        scaled
        - jnp.mean(scaled, axis=-1, keepdims=True)
        - normed * jnp.mean(scaled * normed, axis=-1, keepdims=True)
    )
    input_grad = (cotangent.astype(jnp.float32) + inv_scale * inner).astype(jnp.bfloat16)
    position = lax.axis_index("tensor")
    zero_index = jnp.zeros((), jnp.int32)
    qkv_bias_full = lax.dynamic_update_slice(
        jnp.zeros((3, D), jnp.float32), qkv_bias_local, (zero_index, position * cols)
    )
    up_bias_full = lax.dynamic_update_slice(
        jnp.zeros((FF,), jnp.float32), up_bias_local, (position * units,)
    )
    qkv_bias_sum, up_bias_sum, bias_total, gain_grad, shift_grad = lax.psum(
        (qkv_bias_full, up_bias_full, bias_sum, gain_local, shift_local), ("dp", "tensor")
    )
    qkv_bias_grad = lax.dynamic_slice(qkv_bias_sum, (zero_index, position * cols), (3, cols))
    up_bias_grad = lax.dynamic_slice(up_bias_sum, (position * units,), (units,))
    qkv_share, out_share, up_share, down_share = (
        lax.psum_scatter(
            qkv_grad.astype(jnp.bfloat16), "dp", scatter_dimension=1, tiled=True
        ).astype(jnp.float32),
        lax.psum_scatter(
            out_grad.astype(jnp.bfloat16), "dp", scatter_dimension=1, tiled=True
        ).astype(jnp.float32),
        lax.psum_scatter(
            up_grad.astype(jnp.bfloat16), "dp", scatter_dimension=0, tiled=True
        ).astype(jnp.float32),
        lax.psum_scatter(
            down_grad.astype(jnp.bfloat16), "dp", scatter_dimension=1, tiled=True
        ).astype(jnp.float32),
    )
    return (
        block_out,
        input_grad,
        gain_grad,
        shift_grad,
        qkv_share,
        qkv_bias_grad,
        out_share,
        bias_total,
        up_share,
        up_bias_grad,
        down_share,
        bias_total,
    )


def solution(mesh):
    return jax.shard_map(
        local,
        mesh=mesh,
        in_specs=(
            P(("dp", "tensor"), None),
            P(),
            P(),
            P(None, None, "tensor"),
            P(None, "tensor"),
            P("tensor", None),
            P(),
            P(None, "tensor"),
            P("tensor"),
            P("tensor", None),
            P(),
            P("dp"),
            P(("dp", "tensor"), None),
        ),
        out_specs=(
            P(("dp", "tensor"), None),
            P(("dp", "tensor"), None),
            P(),
            P(),
            P(None, "dp", "tensor"),
            P(None, "tensor"),
            P("tensor", "dp"),
            P(),
            P("dp", "tensor"),
            P("tensor"),
            P("tensor", "dp"),
            P(),
        ),
        check_vma=False,
    )
```

profile of v0, /device:TPU:8, one launch (start us, length us, event | category | flops | bytes accessed | tf_op | source)
XLA Modules:
  0.0 1215.4 jit_solution(16071413295339281055)
XLA Ops:
  20.2 137.2 %all-gather.3.cloned.1.call-done = bf16[2048,2048]{1,0:T(8,128)(2,1)} async-done(((bf16[512,2048]{1,0:T(8,128)(2,1)}), bf16[2048,2048]{1,0:T(8,128)(2,1)}) %all-gather.3.cloned.1.call-update) | async-done | bytes 8388624 | tf_op jit(solution)/shard_map/all_gather | solution.py:103
  157.4 4.7 convert_reduce_fusion
  165.6 23.5 %fusion.98 = (bf16[3,2048,512]{1,2,0:T(8,128)(2,1)}, f32[3,2048,512]{1,2,0:T(8,128)}) fusion(f32[3,512]{1,0:T(4,128)S(1)} %copy-done.57, bf16[3,2048,512]{2,1,0:T(8,128)(2,1)} %param.36, f32[2048]{0:T(1024)S(1)} %copy-done.58, f32[2048]{0:T(1024)S(1)} %copy-done.51, f32[2048]{0:T(1024)S(1)} %add_rsqrt_fusion, f32[2048]{0:T(1024)S(1)} %broadcast_multiply_fusion, ...), kind=kOutput, calls=%fused_computation.174 | convolution fusion | flops 12916359168 | bytes 33593344 | tf_op jit(solution)/shard_map/tm,cml->ctl/dot_general | solution.py:112
  205.3 14.5 %fusion.2 = (f32[8,512]{1,0:T(8,128)S(1)}, f32[8,512,2048]{2,1,0:T(8,128)}) fusion(pred[512,2048]{1,0:T(8,128)(4,1)S(1)} %copy-done.25, bf16[2048,8,32]{0,2,1:T(8,128)(2,1)S(1)} %slice.472, bf16[2048,8,16]{0,2,1:T(8,128)(2,1)S(1)} %get-tuple-element.173, bf16[2048,8,16]{0,2,1:T(8,128)(2,1)S(1)} %get-tuple-element.172, ...), kind=kOutput, calls=%fused_computation.12 | convolution fusion | flops 1105195008 | bytes 37240832 | tf_op jit(solution)/shard_map/qhd,khd->hqk/dot_general | solution.py:78
  219.8 15.1 %exponential_reduce_fusion = f32[8,512]{1,0:T(8,128)S(1)} fusion(f32[8,512,2048]{2,1,0:T(8,128)} %get-tuple-element.196, f32[8,512]{1,0:T(8,128)S(1)} %get-tuple-element.195, pred[512,2048]{1,0:T(8,128)(4,1)S(1)} %copy-done.25), kind=kLoop, calls=%fused_computation.2 | loop fusion | flops 33550336 | bytes 34635776 | tf_op jit(solution)/shard_map/reduce_sum | solution.py:125
  235.0 11.0 fusion.99
  246.0 11.4 exponential_reduce_fusion.1
  265.0 4.8 fusion.25
  269.8 5.2 exponential_reduce_fusion.3
  275.0 6.3 convolution_convert_fusion.5
  281.3 5.4 convolution_convert_fusion.4
  286.7 11.1 fusion.64
  297.7 16.1 %convolution_convert_fusion.6 = bf16[8,64,512]{2,1,0:T(8,128)(2,1)} fusion(bf16[2048,8,64]{0,2,1:T(8,128)(2,1)} %bitcast.164, f32[8,512,2048]{2,1,0:T(8,128)} %get-tuple-element.196, f32[8,512]{1,0:T(8,128)S(1)} %log_add_fusion, pred[512,2048]{1,0:T(8,128)(4,1)} %fusion.38), kind=kOutput, calls=%fused_computation.113 | convolution fusion | flops 1107558400 | bytes 37240832 | tf_op jit(solution)/shard_map/hqk,khd->qhd/dot_general | solution.py:128
  313.9 8.7 convolution_convert_fusion.3
  324.2 5.7 convolution_bitcast_fusion.1
  339.6 4.8 fusion.55
  346.4 10.1 multiply_convert_fusion.2
  360.2 4.5 fusion.56
  364.7 13.3 %fusion.51 = f32[2048,8,64]{0,2,1:T(8,128)} fusion(f32[2048,8,64]{0,2,1:T(8,128)} %copy-done.12, bf16[512,8,64]{0,2,1:T(8,128)(2,1)S(1)} %bitcast.160, f32[8,512,1536]{2,1,0:T(8,128)} %get-tuple-element.198, f32[8,512]{1,0:T(8,128)S(1)} %log_add_fusion.1), kind=kOutput, calls=%fused_computation.85 | convolution fusion | flops 818675712 | bytes 31997952 | tf_op jit(solution)/shard_map/hqk,qhd->khd/dot_general | solution.py:180
  378.1 15.7 %multiply_convert_fusion.1 = bf16[8,512,1536]{2,1,0:T(8,128)(2,1)} fusion(f32[8,512,1536]{2,1,0:T(8,128)} %get-tuple-element.198, bf16[512,8,64]{0,2,1:T(8,128)(2,1)S(1)} %bitcast.161, bf16[1536,8,64]{0,2,1:T(8,128)(2,1)} %bitcast.155, f32[8,512]{1,0:T(8,128)S(1)} %get-tuple-element.178, f32[8,512]{1,0:T(8,128)S(1)} %log_add_fusion.1), kind=kOutput, calls=%fused_computation.6 | convolution fusion | flops 836763648 | bytes 39878656 | tf_op jit(solution)/shard_map/qhd,khd->hqk/dot_general | solution.py:182
  393.7 9.9 fusion.61
  403.6 9.6 fusion.44
  413.2 17.8 %bitcast_add_fusion.1 = f32[2048,8,64]{0,2,1:T(8,128)} fusion(f32[2048,8,64]{0,2,1:T(8,128)} %fusion.51, bf16[512,8,64]{0,2,1:T(8,128)(2,1)} %bitcast.173, f32[8,512,2048]{2,1,0:T(8,128)} %get-tuple-element.196, f32[8,512]{1,0:T(8,128)S(1)} %log_add_fusion, pred[512,2048]{1,0:T(8,128)(4,1)S(1)} %copy-done.26), kind=kOutput, calls=%fused_computation.71 | convolution fusion | flops 1108344832 | bytes 43532288 | tf_op jit(solution)/shard_map/hqk,qhd->khd/dot_general | solution.py:180
  431.0 23.1 %multiply_convert_fusion = bf16[8,512,2048]{2,1,0:T(8,128)(2,1)} fusion(f32[8,512,2048]{2,1,0:T(8,128)} %get-tuple-element.196, bf16[512,8,64]{0,2,1:T(8,128)(2,1)} %bitcast.174, bf16[2048,8,64]{0,2,1:T(8,128)(2,1)} %bitcast.165, f32[8,512]{1,0:T(8,128)S(1)} %get-tuple-element.160, f32[8,512]{1,0:T(8,128)S(1)} %log_add_fusion, pred[512,2048]{1,0:T(8,128)(4,1)} %fusion.38), kind=kOutput, calls=%fused_computation | convolution fusion | flops 1132462080 | bytes 54034432 | tf_op jit(solution)/shard_map/qhd,khd->hqk/dot_general | solution.py:182
  454.1 12.3 %convolution_bitcast_fusion.5 = f32[512,8,64]{0,2,1:T(8,128)} fusion(bf16[8,512,2048]{2,1,0:T(8,128)(2,1)} %multiply_convert_fusion, bf16[2048,8,32]{0,2,1:T(8,128)(2,1)S(1)} %copy-done.10, bf16[2048,8,16]{0,2,1:T(8,128)(2,1)} %copy-done.18, bf16[2048,8,16]{0,2,1:T(8,128)(2,1)} %copy-done.17), kind=kOutput, calls=%fused_computation.109 | convolution fusion | flops 1080033280 | bytes 19922944 | tf_op jit(solution)/shard_map/hqk,khd->qhd/dot_general | solution.py:190
  466.4 10.3 bitcast_add_fusion.2
  480.3 9.2 convolution_convert_fusion.2
  498.0 5.6 copy.44
  503.5 5.5 copy.43
  509.0 5.4 copy.42
  514.4 23.8 %convert_bitcast_fusion = bf16[3,2048,512]{1,2,0:T(8,128)(2,1)} fusion(f32[1,2048,512]{2,1,0:T(8,128)} %copy.44, f32[1,2048,512]{2,1,0:T(8,128)} %copy.43, f32[1,2048,512]{2,1,0:T(8,128)} %copy.42, f32[2048]{0:T(1024)S(1)} %copy-done.59, f32[2048]{0:T(1024)S(1)} %copy-done.52, f32[2048]{0:T(1024)S(1)} %copy-done.49, f32[2048]{0:T(1024)S(1)} %copy-done.46, ...), kind=kOutput, calls=%fused_computation.50 | convolution fusion | flops 12919504896 | bytes 27295744 | tf_op jit(solution)/shard_map/tm,ctl->cml/dot_general | solution.py:204
  538.4 24.7 %fusion.95 = f32[2048,2048]{1,0:T(8,128)} fusion(bf16[2048,2048]{1,0:T(8,128)(2,1)} %param.40, f32[2048]{0:T(1024)S(1)} %copy-done.59, f32[2048]{0:T(1024)S(1)} %copy-done.52, f32[2048]{0:T(1024)S(1)} %copy-done.49, f32[2048]{0:T(1024)S(1)} %copy-done.46, bf16[2048,2048]{1,0:T(8,128)(2,1)} %all-gather.3.cloned.1.call-done), kind=kOutput, calls=%fused_computation.171 | convolution fusion | flops 17205035008 | bytes 33587200 | tf_op jit(solution)/shard_map/dot_general | solution.py:136
  563.1 35.8 %fusion.100 = (f32[2048]{0:T(1024)}, bf16[2048,2048]{1,0:T(8,128)(2,1)}) fusion(f32[2048,2048]{1,0:T(8,128)} %fusion.95, f32[2048]{0:T(1024)S(1)} %copy-done.60, bf16[2048,2048]{1,0:T(8,128)(2,1)} %all-gather.5.cloned.1.call-done, bf16[2048,2048]{1,0:T(8,128)(2,1)} %param.42), kind=kOutput, calls=%fused_computation.176 | convolution fusion | flops 17267947520 | bytes 41959424 | tf_op jit(solution)/shard_map/dot_general | solution.py:159
  598.9 25.2 %convolution_convert_fusion.1 = bf16[2048,2048]{1,0:T(8,128)(2,1)} fusion(bf16[2048,2048]{1,0:T(8,128)(2,1)} %get-tuple-element.204, f32[2048]{0:T(1024)S(1)} %copy-done.59, f32[2048]{0:T(1024)S(1)} %copy-done.52, f32[2048]{0:T(1024)S(1)} %copy-done.49, f32[2048]{0:T(1024)S(1)} %copy-done.46, bf16[2048,2048]{1,0:T(8,128)(2,1)} %all-gather.3.cloned.1.call-done), kind=kOutput, calls=%fused_computation.48 | convolution fusion | flops 17209229312 | bytes 25198592 | tf_op jit(solution)/shard_map/dot_general | solution.py:164
  624.1 27.1 %convolution_convert_fusion = bf16[2048,2048]{1,0:T(8,128)(2,1)} fusion(bf16[2048,2048]{1,0:T(8,128)(2,1)} %all-gather.5.cloned.1.call-done, f32[2048,2048]{1,0:T(8,128)} %fusion.95, f32[2048]{0:T(1024)S(1)} %copy-done.60), kind=kOutput, calls=%fused_computation.47 | convolution fusion | flops 17226006528 | bytes 33562624 | tf_op jit(solution)/shard_map/dot_general | solution.py:154
  651.3 20.5 %fusion.93 = f32[2048,2048,1]{1,0,2:T(8,128)} fusion(bf16[3,2048,512]{2,1,0:T(8,128)(2,1)} %param.36, f32[1,2048,512]{2,1,0:T(8,128)} %copy.44, f32[1,2048,512]{2,1,0:T(8,128)} %copy.43, f32[1,2048,512]{2,1,0:T(8,128)} %copy.42), kind=kOutput, calls=%fused_computation.170 | convolution fusion | flops 12891193344 | bytes 35651584 | tf_op jit(solution)/shard_map/crl,cml->rm/dot_general | solution.py:208
  671.7 25.6 %fusion.12 = bf16[2048,2048]{1,0:T(8,128)(2,1)} fusion(f32[2048,2048,1]{1,0,2:T(8,128)} %fusion.93, bf16[2048,2048]{1,0:T(8,128)(2,1)} %param.40, bf16[2048,2048]{1,0:T(8,128)(2,1)} %get-tuple-element.204), kind=kOutput, calls=%fused_computation.25 | convolution fusion | flops 17188257792 | bytes 41943040 | tf_op jit(solution)/shard_map/dot_general | solution.py:214
  697.4 11.0 fusion.101
  708.4 31.0 %add_convert_fusion = bf16[2048,2048]{1,0:T(8,128)(2,1)} fusion(f32[2048,2048]{1,0:T(8,128)} %fusion.101, bf16[2048,2048]{1,0:T(8,128)(2,1)} %param.42, f32[2048,2048]{1,0:T(8,128)} %fusion.95, f32[2048]{0:T(1024)S(1)} %copy-done.60), kind=kOutput, calls=%fused_computation.27 | convolution fusion | flops 17230200832 | bytes 50339840 | tf_op jit(solution)/shard_map/dot_general | solution.py:143
  740.7 5.3 fusion.15
  746.0 11.4 fusion.3
  764.6 6.7 reduce-scatter.17.cloned.1.call-done
  774.1 143.9 %reduce-scatter.9.cloned.1.call-done = bf16[512,2048]{1,0:T(8,128)(2,1)} async-done(((bf16[2048,2048]{1,0:T(8,128)(2,1)}), bf16[512,2048]{1,0:T(8,128)(2,1)}) %reduce-scatter.9.cloned.1.call-update) | async-done | bytes 2097168 | tf_op jit(solution)/shard_map/reduce_scatter | solution.py:211
  918.0 5.0 fusion.34
  923.0 6.0 convert_reduce_fusion.2
  928.9 136.6 %reduce-scatter.7.cloned.1.call-done = bf16[512,2048]{1,0:T(8,128)(2,1)} async-done(((bf16[2048,2048]{1,0:T(8,128)(2,1)}), bf16[512,2048]{1,0:T(8,128)(2,1)}) %reduce-scatter.7.cloned.1.call-update) | async-done | bytes 2097168 | tf_op jit(solution)/shard_map/reduce_scatter | solution.py:140
  1065.6 4.6 add_convert_fusion.2
  1070.1 130.8 %all-reduce.5.cloned.1.call-done = (f32[2048]{0:T(1024)}, f32[2048]{0:T(1024)}, f32[3,2048]{1,0:T(4,128)}, f32[2048]{0:T(1024)}, f32[8192]{0:T(1024)}) async-done(((f32[2048]{0:T(1024)}, f32[2048]{0:T(1024)}, f32[3,2048]{1,0:T(4,128)}, f32[2048]{0:T(1024)}, f32[8192]{0:T(1024)}), (f32[2048]{0:T(1024)}, f32[2048]{0:T(1024)}, f32[3,2048]{1,0:T(4,128)}, f32[2048]{0:T(1024)}, ...) | async-done | bytes 81936 | tf_op jit(solution)/shard_map/psum | solution.py:239
  (225 shorter events, 88.1 us)
Async XLA Ops:
  7.2 306.7 %copy-start = (bf16[512,2048]{1,0:T(8,128)(2,1)S(1)}, bf16[512,2048]{1,0:T(8,128)(2,1)}, u32[]{:S(2)}) copy-start(bf16[512,2048]{1,0:T(8,128)(2,1)} %param.38) | copy-start | bytes 6291460
  7.2 150.2 %all-gather.3.cloned.1.call-start = ((), (), s32[]{:S(2)}) async-start(), calls=%async_computation.6 | async-start | bytes 10485760 | tf_op jit(solution)/shard_map/all_gather | solution.py:103
  7.9 305.9 %all-gather.5.cloned.1.call-start = ((), (), s32[]{:S(2)}) async-start(), calls=%async_computation.8 | async-start | bytes 10485760 | tf_op jit(solution)/shard_map/all_gather | solution.py:151
  8.7 748.8 %reduce-scatter.13.cloned.1.call-start = ((), (), s32[]{:S(2)}) async-start(), calls=%async_computation.11 | async-start | bytes 2359296 | tf_op jit(solution)/shard_map/reduce_scatter | solution.py:248
  20.2 145.3 %copy-start.51 = (f32[2048]{0:T(1024)S(1)}, f32[2048]{0:T(1024)}, u32[]{:S(2)}) copy-start(f32[2048]{0:T(1024)} %param.34) | copy-start | bytes 24580
  20.2 145.3 %copy-start.57 = (f32[3,512]{1,0:T(4,128)S(1)}, f32[3,512]{1,0:T(4,128)}, u32[]{:S(2)}) copy-start(f32[3,512]{1,0:T(4,128)} %param.37) | copy-start | bytes 18436
  20.2 145.3 %copy-start.58 = (f32[2048]{0:T(1024)S(1)}, f32[2048]{0:T(1024)}, u32[]{:S(2)}) copy-start(f32[2048]{0:T(1024)} %param.35) | copy-start | bytes 24580
  163.2 25.8 %copy-start.45 = (f32[2048]{0:T(1024)}, f32[2048]{0:T(1024)S(1)}, u32[]{:S(2)}) copy-start(f32[2048]{0:T(1024)S(1)} %broadcast_multiply_fusion) | copy-start | bytes 24580
  165.5 23.5 %copy-start.48 = (f32[2048]{0:T(1024)}, f32[2048]{0:T(1024)S(1)}, u32[]{:S(2)}) copy-start(f32[2048]{0:T(1024)S(1)} %add_rsqrt_fusion) | copy-start | bytes 24580
  193.7 93.0 %copy-start.11 = (bf16[1,1536,512]{1,2,0:T(8,128)(2,1)}, bf16[1,1536,512]{1,2,0:T(8,128)(2,1)S(1)}, u32[]{:S(2)}) copy-start(bf16[1,1536,512]{1,2,0:T(8,128)(2,1)S(1)} %slice.411) | copy-start | bytes 4718596
  203.5 16.3 %copy-start.17 = (bf16[2048,8,16]{0,2,1:T(8,128)(2,1)}, bf16[2048,8,16]{0,2,1:T(8,128)(2,1)S(1)}, u32[]{:S(2)}) copy-start(bf16[2048,8,16]{0,2,1:T(8,128)(2,1)S(1)} %get-tuple-element.172) | copy-start | bytes 1572868
  203.5 16.3 %copy-start.18 = (bf16[2048,8,16]{0,2,1:T(8,128)(2,1)}, bf16[2048,8,16]{0,2,1:T(8,128)(2,1)S(1)}, u32[]{:S(2)}) copy-start(bf16[2048,8,16]{0,2,1:T(8,128)(2,1)S(1)} %get-tuple-element.173) | copy-start | bytes 1572868
  204.9 52.5 %copy-start.3 = (bf16[2048,8,64]{0,2,1:T(8,128)(2,1)}, bf16[2048,8,64]{0,2,1:T(8,128)(2,1)S(1)}, u32[]{:S(2)}) copy-start(bf16[2048,8,64]{0,2,1:T(8,128)(2,1)S(1)} %get-tuple-element.206) | copy-start | bytes 6291460
  204.9 60.0 %copy-start.5 = (bf16[2048,8,64]{0,2,1:T(8,128)(2,1)}, bf16[2048,8,64]{0,2,1:T(8,128)(2,1)S(1)}, u32[]{:S(2)}) copy-start(bf16[2048,8,64]{0,2,1:T(8,128)(2,1)S(1)} %get-tuple-element.205) | copy-start | bytes 6291460
  219.8 15.2 %copy-start.19 = (pred[512,1536]{1,0:T(8,128)(4,1)S(1)}, pred[512,1536]{1,0:T(8,128)(4,1)}, u32[]{:S(2)}) copy-start(pred[512,1536]{1,0:T(8,128)(4,1)} %fusion.54) | copy-start | bytes 2359300
  246.0 11.4 copy-start.20
  260.5 20.9 %copy-start.2 = (f32[8,512,1024]{2,1,0:T(8,128)}, f32[8,512,1024]{2,1,0:T(8,128)S(1)}, u32[]{:S(2)}) copy-start(f32[8,512,1024]{2,1,0:T(8,128)S(1)} %get-tuple-element.200) | copy-start | bytes 50331652
  265.0 10.0 copy-start.41
  269.8 11.6 copy-start.39
  313.9 8.8 copy-start.29
  329.9 9.6 slice-start
  329.9 9.6 slice-start.1
  346.4 10.1 copy-start.4
  403.6 9.6 copy-start.26
  431.0 23.1 %copy-start.10 = (bf16[2048,8,32]{0,2,1:T(8,128)(2,1)S(1)}, bf16[2048,8,32]{0,2,1:T(8,128)(2,1)}, u32[]{:S(2)}) copy-start(bf16[2048,8,32]{0,2,1:T(8,128)(2,1)} %copy-done.9) | copy-start | bytes 3145732
  466.4 12.3 %copy-start.22 = (bf16[8,64,512]{2,1,0:T(8,128)(2,1)S(1)}, bf16[8,64,512]{2,1,0:T(8,128)(2,1)}, u32[]{:S(2)}) copy-start(bf16[8,64,512]{2,1,0:T(8,128)(2,1)} %fusion.64) | copy-start | bytes 1572868
  466.4 12.3 %copy-start.30 = (bf16[8,64,512]{2,1,0:T(8,128)(2,1)S(1)}, bf16[8,64,512]{2,1,0:T(8,128)(2,1)}, u32[]{:S(2)}) copy-start(bf16[8,64,512]{2,1,0:T(8,128)(2,1)} %convolution_convert_fusion.5) | copy-start | bytes 1572868
  466.4 12.3 %copy-start.32 = (bf16[8,64,512]{2,1,0:T(8,128)(2,1)S(1)}, bf16[8,64,512]{2,1,0:T(8,128)(2,1)}, u32[]{:S(2)}) copy-start(bf16[8,64,512]{2,1,0:T(8,128)(2,1)} %convolution_convert_fusion.4) | copy-start | bytes 1572868
  466.4 12.3 %copy-start.34 = (bf16[8,64,512]{2,1,0:T(8,128)(2,1)S(1)}, bf16[8,64,512]{2,1,0:T(8,128)(2,1)}, u32[]{:S(2)}) copy-start(bf16[8,64,512]{2,1,0:T(8,128)(2,1)} %convolution_convert_fusion.6) | copy-start | bytes 1572868
  480.3 9.7 copy-start.13
  480.3 9.7 copy-start.36
  480.3 9.7 copy-start.38
  489.5 269.7 %reduce-scatter.11.cloned.1.call-start = ((), (), s32[]{:S(2)}) async-start(), calls=%async_computation.10 | async-start | bytes 7077888 | tf_op jit(solution)/shard_map/reduce_scatter | solution.py:245
  503.5 10.9 copy-start.46
  503.5 10.9 copy-start.49
  503.5 10.9 copy-start.52
  503.5 10.9 copy-start.59
  538.2 24.9 %copy-start.60 = (f32[2048]{0:T(1024)S(1)}, f32[2048]{0:T(1024)}, u32[]{:S(2)}) copy-start(f32[2048]{0:T(1024)} %param.41) | copy-start | bytes 24580
  538.2 223.6 %reduce-scatter.15.cloned.1.call-start = ((), (), s32[]{:S(2)}) async-start(), calls=%async_computation.12 | async-start | bytes 9437184 | tf_op jit(solution)/shard_map/reduce_scatter | solution.py:251
  624.1 147.3 %reduce-scatter.17.cloned.1.call-start = ((), (), s32[]{:S(2)}) async-start(), calls=%async_computation.13 | async-start | bytes 9437184 | tf_op jit(solution)/shard_map/reduce_scatter | solution.py:254
  651.2 266.7 %reduce-scatter.9.cloned.1.call-start = ((), (), s32[]{:S(2)}) async-start(), calls=%async_computation.9 | async-start | bytes 10485760 | tf_op jit(solution)/shard_map/reduce_scatter | solution.py:211
  697.4 368.2 %reduce-scatter.7.cloned.1.call-start = ((), (), s32[]{:S(2)}) async-start(), calls=%async_computation.7 | async-start | bytes 10485760 | tf_op jit(solution)/shard_map/reduce_scatter | solution.py:140
  739.5 461.4 %all-reduce.5.cloned.1.call-start = ((), (), s32[]{:S(2)}) async-start(), calls=%async_computation.14 | async-start | bytes 180224 | tf_op jit(solution)/shard_map/psum | solution.py:239
  740.7 16.8 %copy-start.44 = (f32[8192]{0:T(1024)}, f32[8192]{0:T(1024)S(1)}, u32[]{:S(2)}) copy-start(f32[8192]{0:T(1024)S(1)} %dynamic_update_slice.7) | copy-start | bytes 98308
  746.0 11.5 copy-start.43
  757.5 160.5 %copy-start.53 = (f32[2048]{0:T(1024)S(1)}, f32[2048]{0:T(1024)}, u32[]{:S(2)}) copy-start(f32[2048]{0:T(1024)} %param.34) | copy-start | bytes 24580
  774.1 291.5 %copy-start.54 = (f32[2048]{0:T(1024)S(1)}, f32[2048]{0:T(1024)}, u32[]{:S(2)}) copy-start(f32[2048]{0:T(1024)} %param.43) | copy-start | bytes 24580
  774.1 291.5 %copy-start.55 = (f32[2048]{0:T(1024)S(1)}, f32[2048]{0:T(1024)}, u32[]{:S(2)}) copy-start(f32[2048]{0:T(1024)} %param.39) | copy-start | bytes 24580
  (29 other events, 127.5 us)
Sparse Core Ops, SparseCore 0:
  9.6 147.8 all-gather.2
  159.0 147.7 all-gather.4
  489.7 42.1 reduce-scatter.12
  538.3 62.7 reduce-scatter.10
  624.2 72.4 reduce-scatter.14
  700.1 71.2 reduce-scatter.16
  773.7 144.2 reduce-scatter.8
  920.3 145.1 reduce-scatter.6
  1073.1 127.7 all-reduce.4
where the time goes:
time: 1220 us
  waiting for transfers between devices  557 us (46%)
  matrix products  485 us (40%)
  other arithmetic  104 us (9%)
  local copies, waits for them, and re-layouts  53.7 us (4%)
  between operations  14.9 us (1%)
    reduce_scatter x1, waiting for transfers between devices, local(): lax.psum_scatter((term + lax.dot_general(rows_act, up_weight, contract_co...  144 us
    all_gather x1, waiting for transfers between devices, local(): whole_in = lax.all_gather(block_in, 'tensor', axis=0, tiled=True)  137 us
    reduce_scatter x1, waiting for transfers between devices, local(): lax.psum_scatter((jnp.dot(attended_flat, out_weight, preferred_element_ty...  137 us
    psum x1, waiting for transfers between devices, local(): lax.psum((qkv_bias_full, up_bias_full, bias_sum, gain_local, shift_local)...  131 us
    dot_general x4, matrix products, local(): jnp.einsum('qhd,khd->hqk', grad_rows, value[:end], preferred_element_type...  52.2 us
    dot_general x4, matrix products, local(): jnp.einsum('hqk,qhd->khd', probs, grad_rows, preferred_element_type=jnp.f...  41.6 us
    dot_general x4, matrix products, local(): jnp.einsum('hqk,khd->qhd', probs, value[:end], preferred_element_type=jnp...  38.8 us
    reduce_sum x4, other arithmetic, local(): jnp.sum(jnp.exp(scores - peak), axis=-1, keepdims=True)  36.1 us
  transfers between devices with their start and end apart: 9, of which 5 were waited for; matrix products, arithmetic and copies ran while one was open for 38% of the time, Pallas kernels for 0%

commit v1 on v0

v1 whole, which is shorter than its diff:
```python
import functools

import jax
import jax.numpy as jnp
from jax import lax
from jax.experimental import pallas as pl
from jax.experimental.pallas import tpu as pltpu
from jax.sharding import PartitionSpec as P

HD = 64
ROT = 32

EPSILON = 1e-05
NEGATIVE = -1e30
ROOT_TWO_PI = 0.7978845608028654
MESH = pl.DeviceIdType.MESH


def normalize(rows):
    wide = rows.astype(jnp.float32)
    centre = wide - jnp.mean(wide, axis=-1, keepdims=True)
    inv_scale = lax.rsqrt(jnp.mean(centre * centre, axis=-1, keepdims=True) + EPSILON)
    return (centre * inv_scale, inv_scale)


def gelu_pair(pre):
    inner = ROOT_TWO_PI * (pre + 0.044715 * pre * pre * pre)
    tangent = jnp.tanh(inner)
    value = 0.5 * pre * (1.0 + tangent)
    slope = 0.5 * (1.0 + tangent) + 0.5 * pre * (1.0 - tangent * tangent) * ROOT_TWO_PI * (
        1.0 + 3.0 * 0.044715 * pre * pre
    )
    return (value, slope)


def sum_kernel(axes, x_ref, out_ref, *scratch):
    barrier = pltpu.get_barrier_semaphore()
    peers = 0
    for name, size in axes:
        me = lax.axis_index(name)
        for step in range(1, size):
            pl.semaphore_signal(
                barrier, inc=1, device_id={name: lax.rem(me + step, size)}, device_id_type=MESH
            )
            peers += 1
    pl.semaphore_wait(barrier, peers)
    held = x_ref
    for number, (name, size) in enumerate(axes):
        slots, total, send, receive = scratch[4 * number : 4 * number + 4]
        me = lax.axis_index(name)
        copies = []
        for step in range(1, size):
            copy = pltpu.make_async_remote_copy(
                src_ref=held,
                dst_ref=slots.at[step - 1],
                send_sem=send.at[step - 1],
                recv_sem=receive.at[step - 1],
                device_id={name: lax.rem(me + step, size)},
                device_id_type=MESH,
            )
            copy.start()
            copies.append(copy)
        for copy in copies:
            copy.wait()
        made = jnp.zeros(x_ref.shape, jnp.float32)
        for device in range(size):
            piece = jnp.where(me == device, held[...], 0.0)
            for step in range(1, size):
                piece = piece + jnp.where(
                    lax.rem(me + size - step, size) == device, slots[step - 1], 0.0
                )
            made = made + piece
        total[...] = made
        held = total
    out_ref[...] = held[...]


def small_sum(values, axes, collective_id):
    scratch = []
    for _, size in axes:
        scratch += [
            pltpu.VMEM((size - 1, *values.shape), jnp.float32),
            pltpu.VMEM(values.shape, jnp.float32),
            pltpu.SemaphoreType.DMA((size - 1,)),
            pltpu.SemaphoreType.DMA((size - 1,)),
        ]
    return pl.pallas_call(
        functools.partial(sum_kernel, axes),
        out_shape=jax.ShapeDtypeStruct(values.shape, jnp.float32),
        in_specs=[pl.BlockSpec(memory_space=pltpu.VMEM)],
        out_specs=pl.BlockSpec(memory_space=pltpu.VMEM),
        scratch_shapes=scratch,
        compiler_params=pltpu.CompilerParams(collective_id=collective_id, has_side_effects=True),
        name="small_sum",
    )(values)


def lanes_of(*parts):
    return jnp.concatenate([part.reshape(-1, 128) for part in parts], axis=0)


LOG2E = 1.4426950408889634
BLOCK = 256


def attention_bounds(segments):
    length = segments.shape[0]
    begins = jnp.sum(
        (segments[None, :] < jnp.arange(1, 4, dtype=jnp.int32)[:, None]).astype(jnp.int32), axis=1
    )
    start = jnp.zeros_like(segments)
    for number in range(1, 4):
        start = jnp.where(segments == number, begins[number - 1], start)
    blocks = length // BLOCK
    rows = start.reshape(blocks, BLOCK)
    low, high = rows[:, 0], rows[:, BLOCK - 1]
    index = jnp.arange(blocks, dtype=jnp.int32)
    key_first = low // BLOCK
    key_whole = jnp.minimum((high + BLOCK - 1) // BLOCK, index)
    later = index[None, :] > index[:, None]
    query_whole = index + 1 + jnp.sum(
        (later & (high[None, :] <= index[:, None] * BLOCK)).astype(jnp.int32), axis=1
    )
    query_last = index + 1 + jnp.sum(
        (later & (low[None, :] < (index[:, None] + 1) * BLOCK)).astype(jnp.int32), axis=1
    )
    return start, jnp.stack([key_first, key_whole, query_whole, query_last])


def head_rows(values, head):
    row = lax.broadcasted_iota(jnp.int32, values.shape, 0)
    return jnp.where(row // HD == head, values, jnp.zeros_like(values))


def head_lanes(values, head):
    lane = lax.broadcasted_iota(jnp.int32, values.shape, 1)
    return jnp.where(lane // HD == head, values, jnp.zeros_like(values))


def allowed_tile(start_row, key_block, query_block):
    shape = (BLOCK, BLOCK)
    key_index = key_block * BLOCK + lax.broadcasted_iota(jnp.int32, shape, 0)
    query_index = query_block * BLOCK + lax.broadcasted_iota(jnp.int32, shape, 1)
    return (key_index <= query_index) & (key_index >= start_row)


def forward_kernel(bounds, start_ref, q_ref, k_ref, v_ref, out_ref, lse_ref, vt_ref):
    i = pl.program_id(1)
    blocks = k_ref.shape[0] // BLOCK

    @pl.when(i == 0)
    def _():
        for b in range(blocks):
            vt_ref[:, b * BLOCK : (b + 1) * BLOCK] = v_ref[b * BLOCK : (b + 1) * BLOCK, :].T

    query = q_ref[...].T
    queries = [head_rows(query, head) for head in range(2)]
    start_row = start_ref[...]

    def step(masked):
        def body(j, carry):
            at = pl.ds(pl.multiple_of(j * BLOCK, BLOCK), BLOCK)
            key = k_ref[at, :]
            new = []
            if masked:
                allowed = allowed_tile(start_row, j, i)
            for head in range(2):
                peak, total, acc = carry[head]
                scores = jnp.dot(key, queries[head], preferred_element_type=jnp.float32)
                scores = scores * (HD**-0.5 * LOG2E)
                if masked:
                    scores = jnp.where(allowed, scores, NEGATIVE)
                top = jnp.maximum(peak, jnp.max(scores, axis=0, keepdims=True))
                probs = jnp.exp2(scores - top)
                shrink = jnp.exp2(peak - top)
                total = total * shrink + jnp.sum(probs, axis=0, keepdims=True)
                acc = acc * shrink + jnp.dot(
                    vt_ref[head * HD : (head + 1) * HD, at],
                    probs.astype(jnp.bfloat16),
                    preferred_element_type=jnp.float32,
                )
                new.append((top, total, acc))
            return tuple(new)

        return body

    carry = tuple(
        (
            jnp.full((1, BLOCK), NEGATIVE, jnp.float32),
            jnp.zeros((1, BLOCK), jnp.float32),
            jnp.zeros((HD, BLOCK), jnp.float32),
        )
        for _ in range(2)
    )
    first, whole = bounds[0, i], bounds[1, i]
    carry = lax.fori_loop(first, whole, step(True), carry)
    carry = lax.fori_loop(jnp.maximum(whole, first), i, step(False), carry)
    carry = step(True)(i, carry)
    rows = [acc / total for _, total, acc in carry]
    out_ref[...] = jnp.concatenate(rows, axis=0).T.astype(jnp.bfloat16)
    lse_ref[0] = jnp.concatenate([top + jnp.log2(total) for top, total, _ in carry], axis=0)


def attention_forward(bounds, start, query, key, value):
    length, cols = query.shape
    pairs, blocks = cols // (2 * HD), length // BLOCK
    width = 2 * HD
    whole = pl.BlockSpec((length, width), lambda p, i, b: (0, p))
    block = pl.BlockSpec((BLOCK, width), lambda p, i, b: (i, p))
    return pl.pallas_call(
        forward_kernel,
        out_shape=(
            jax.ShapeDtypeStruct((length, cols), jnp.bfloat16),
            jax.ShapeDtypeStruct((pairs, 2, length), jnp.float32),
        ),
        grid_spec=pltpu.PrefetchScalarGridSpec(
            num_scalar_prefetch=1,
            grid=(pairs, blocks),
            in_specs=[pl.BlockSpec((1, BLOCK), lambda p, i, b: (0, i)), block, whole, whole],
            out_specs=(block, pl.BlockSpec((1, 2, BLOCK), lambda p, i, b: (p, 0, i))),
            scratch_shapes=[pltpu.VMEM((width, length), jnp.bfloat16)],
        ),
        compiler_params=pltpu.CompilerParams(dimension_semantics=("arbitrary", "arbitrary")),
        cost_estimate=pl.CostEstimate(
            flops=16 * 10**9, bytes_accessed=4 * 2 * length * cols, transcendentals=0
        ),
        name="attention_forward",
    )(bounds, start.reshape(1, length), query, key, value)


def turn(values, cosine, sine, sign):
    lane = lax.broadcasted_iota(jnp.int32, values.shape, 1)
    half = ROT // 2
    right = pltpu.roll(values, half, 1)
    left = pltpu.roll(values, values.shape[1] - half, 1)
    mixed = jnp.where(lane % HD < half, -left, right)
    return values * cosine + (sign * mixed) * sine


def backward_kernel(
    bounds, start_ref, cos_ref, sin_ref, q_ref, k_ref, v_ref, out_ref, grad_ref, lse_ref,
    dq_ref, dk_ref, dv_ref, bias_ref, dqt_ref, qt_ref, gt_ref, delta_ref,
):
    j = pl.program_id(1)
    blocks = q_ref.shape[0] // BLOCK

    @pl.when(j == 0)
    def _():
        bias_ref[...] = jnp.zeros_like(bias_ref)
        dqt_ref[...] = jnp.zeros_like(dqt_ref)

        @pl.loop(0, blocks)
        def _(i):
            at = pl.ds(pl.multiple_of(i * BLOCK, BLOCK), BLOCK)
            grad = grad_ref[at, :]
            qt_ref[:, at] = q_ref[at, :].T
            gt_ref[:, at] = grad.T
            both = (grad.astype(jnp.float32) * out_ref[at, :].astype(jnp.float32)).T
            delta_ref[:, at] = jnp.concatenate(
                [
                    jnp.sum(both[head * HD : (head + 1) * HD], axis=0, keepdims=True)
                    for head in range(2)
                ],
                axis=0,
            )

    key, value = k_ref[...], v_ref[...]
    key_t = key.T
    width = key.shape[1]

    def step(masked):
        def body(i, carry):
            at = pl.ds(pl.multiple_of(i * BLOCK, BLOCK), BLOCK)
            key_grad, value_grad = carry
            query, grad = q_ref[at, :], grad_ref[at, :]
            query_t, grad_t = qt_ref[:, at], gt_ref[:, at]
            if masked:
                allowed = allowed_tile(start_ref[:, at], j, i)
            for head in range(2):
                scores = jnp.dot(key, head_rows(query_t, head), preferred_element_type=jnp.float32)
                probs = jnp.exp2(
                    scores * (HD**-0.5 * LOG2E) - lse_ref[0, head : head + 1, at]
                )
                if masked:
                    probs = jnp.where(allowed, probs, 0.0)
                back = jnp.dot(value, head_rows(grad_t, head), preferred_element_type=jnp.float32)
                score_grad = (probs * (back - delta_ref[head : head + 1, at])).astype(jnp.bfloat16)
                value_grad = value_grad + jnp.dot(
                    probs.astype(jnp.bfloat16), head_lanes(grad, head), preferred_element_type=jnp.float32
                )
                key_grad = key_grad + jnp.dot(
                    score_grad, head_lanes(query, head), preferred_element_type=jnp.float32
                )
                dqt_ref[head * HD : (head + 1) * HD, at] += jnp.dot(
                    key_t[head * HD : (head + 1) * HD], score_grad, preferred_element_type=jnp.float32
                )
            return key_grad, value_grad

        return body

    zero = jnp.zeros((BLOCK, width), jnp.float32)
    whole, last = bounds[2, j], bounds[3, j]
    carry = step(True)(j, (zero, zero))
    carry = lax.fori_loop(j + 1, whole, step(False), carry)
    key_grad, value_grad = lax.fori_loop(whole, last, step(True), carry)
    here = pl.ds(pl.multiple_of(j * BLOCK, BLOCK), BLOCK)
    key_grad = turn(key_grad * HD**-0.5, cos_ref[here, :], sin_ref[here, :], -1.0)
    dk_ref[...] = key_grad.astype(jnp.bfloat16)
    dv_ref[...] = value_grad.astype(jnp.bfloat16)
    bias_ref[1:2, :] += jnp.sum(key_grad, axis=0, keepdims=True)
    bias_ref[2:3, :] += jnp.sum(value_grad, axis=0, keepdims=True)

    @pl.when(j == blocks - 1)
    def _():
        @pl.loop(0, blocks)
        def _(i):
            at = pl.ds(pl.multiple_of(i * BLOCK, BLOCK), BLOCK)
            query_grad = turn(dqt_ref[:, at].T * HD**-0.5, cos_ref[at, :], sin_ref[at, :], -1.0)
            dq_ref[at, :] = query_grad.astype(jnp.bfloat16)
            bias_ref[0:1, :] += jnp.sum(query_grad, axis=0, keepdims=True)


def attention_backward(bounds, start, cosine, sine, query, key, value, attended, grad, lse):
    length, cols = query.shape
    width = 2 * HD
    pairs, blocks = cols // width, length // BLOCK
    whole = pl.BlockSpec((length, width), lambda p, j, b: (0, p))
    block = pl.BlockSpec((BLOCK, width), lambda p, j, b: (j, p))
    table = pl.BlockSpec((length, width), lambda p, j, b: (0, 0))
    shape = jax.ShapeDtypeStruct((length, cols), jnp.bfloat16)
    return pl.pallas_call(
        backward_kernel,
        out_shape=(shape, shape, shape, jax.ShapeDtypeStruct((3, cols), jnp.float32)),
        grid_spec=pltpu.PrefetchScalarGridSpec(
            num_scalar_prefetch=1,
            grid=(pairs, blocks),
            in_specs=[
                pl.BlockSpec((1, length), lambda p, j, b: (0, 0)),
                table,
                table,
                whole,
                block,
                block,
                whole,
                whole,
                pl.BlockSpec((1, 2, length), lambda p, j, b: (p, 0, 0)),
            ],
            out_specs=(whole, block, block, pl.BlockSpec((3, width), lambda p, j, b: (0, p))),
            scratch_shapes=[
                pltpu.VMEM((width, length), jnp.float32),
                pltpu.VMEM((width, length), jnp.bfloat16),
                pltpu.VMEM((width, length), jnp.bfloat16),
                pltpu.VMEM((2, length), jnp.float32),
            ],
        ),
        compiler_params=pltpu.CompilerParams(dimension_semantics=("arbitrary", "arbitrary")),
        cost_estimate=pl.CostEstimate(
            flops=40 * 10**9, bytes_accessed=8 * 2 * length * cols, transcendentals=0
        ),
        name="attention_backward",
    )(bounds, start.reshape(1, length), cosine, sine, query, key, value, attended, grad, lse)


def project_kernel(hidden_ref, weight_ref, bias_ref, cos_ref, sin_ref, q_ref, k_ref, v_ref):
    hidden = hidden_ref[...]
    width = 2 * HD
    for part, out in enumerate((q_ref, k_ref, v_ref)):
        made = jnp.dot(hidden, weight_ref[part], preferred_element_type=jnp.float32)
        made = made + bias_ref[part : part + 1, :]
        for pair in range(made.shape[1] // width):
            lanes = slice(pair * width, (pair + 1) * width)
            piece = made[:, lanes]
            if part < 2:
                piece = turn(piece, cos_ref[...], sin_ref[...], 1.0)
            out[:, lanes] = piece.astype(jnp.bfloat16)


def project(hidden, weight, bias, cosine, sine):
    rows, depth = hidden.shape
    cols = weight.shape[2]
    width = 2 * HD
    made = jax.ShapeDtypeStruct((rows, cols), jnp.bfloat16)
    table = pl.BlockSpec((BLOCK, width), lambda i: (i, 0))
    out = pl.BlockSpec((BLOCK, cols), lambda i: (i, 0))
    return pl.pallas_call(
        project_kernel,
        out_shape=(made, made, made),
        grid=(rows // BLOCK,),
        in_specs=[
            pl.BlockSpec((BLOCK, depth), lambda i: (i, 0)),
            pl.BlockSpec((3, depth, cols), lambda i: (0, 0, 0)),
            pl.BlockSpec((3, cols), lambda i: (0, 0)),
            table,
            table,
        ],
        out_specs=(out, out, out),
        compiler_params=pltpu.CompilerParams(dimension_semantics=("arbitrary",)),
        cost_estimate=pl.CostEstimate(
            flops=2 * rows * depth * 3 * cols,
            bytes_accessed=2 * (rows * depth + 3 * depth * cols + 3 * rows * cols),
            transcendentals=0,
        ),
        name="project",
    )(hidden, weight, bias, cosine, sine)


def rotary_tables(segments, start):
    length = segments.shape[0]
    place = (jnp.arange(length, dtype=jnp.int32) - start).astype(jnp.float32)
    freq = 10000.0 ** (-(2.0 * jnp.arange(ROT // 2, dtype=jnp.float32)) / ROT)
    lane = jnp.arange(2 * HD, dtype=jnp.int32) % HD
    angle = place[:, None] * jnp.tile(freq, 2 * HD // (ROT // 2))[None, :]
    turned = (lane < ROT)[None, :]
    return jnp.where(turned, jnp.cos(angle), 1.0), jnp.where(turned, jnp.sin(angle), 0.0)


def local(
    sizes,
    block_in,
    ln_gain,
    ln_bias,
    qkv_weight,
    qkv_bias,
    out_weight,
    out_bias,
    up_weight,
    up_bias,
    down_weight,
    down_bias,
    segments,
    cotangent,
):
    dp, tensor = sizes
    depth = block_in.shape[1]
    units = up_weight.shape[1]
    cols = qkv_weight.shape[2]
    contract_rows = (((0,), (0,)), ((), ()))
    contract_cols = (((1,), (1,)), ((), ()))
    normed, inv_scale = normalize(block_in)
    hidden_own = (normed * ln_gain + ln_bias).astype(jnp.bfloat16)
    hidden = lax.all_gather(hidden_own, "tensor", axis=0, tiled=True)
    grad_out = lax.all_gather(cotangent, "tensor", axis=0, tiled=True)
    start, bounds = attention_bounds(segments)
    cosine, sine = rotary_tables(segments, start)
    query, key, value = project(hidden, qkv_weight, qkv_bias, cosine, sine)
    attended, log_sums = attention_forward(bounds, start, query, key, value)
    act_pre = jnp.dot(hidden, up_weight, preferred_element_type=jnp.float32) + up_bias
    act_value, act_slope = gelu_pair(act_pre)
    act = act_value.astype(jnp.bfloat16)
    slope = act_slope.astype(jnp.bfloat16)
    branch = lax.psum_scatter(
        (
            jnp.dot(attended, out_weight, preferred_element_type=jnp.float32)
            + jnp.dot(act, down_weight, preferred_element_type=jnp.float32)
        ).astype(jnp.bfloat16),
        "tensor",
        scatter_dimension=0,
        tiled=True,
    ).astype(jnp.float32)
    block_out = (block_in.astype(jnp.float32) + branch + out_bias + down_bias).astype(jnp.bfloat16)
    bias_sum = jnp.sum(grad_out.astype(jnp.float32), axis=0)
    down_grad = lax.dot_general(
        act, grad_out, contract_rows, preferred_element_type=jnp.float32
    ).astype(jnp.bfloat16)
    act_grad = lax.dot_general(
        grad_out, down_weight, contract_cols, preferred_element_type=jnp.float32
    ) * slope.astype(jnp.float32)
    up_bias_local = jnp.sum(act_grad, axis=0)
    act_grad_b = act_grad.astype(jnp.bfloat16)
    up_grad = lax.dot_general(
        hidden, act_grad_b, contract_rows, preferred_element_type=jnp.float32
    ).astype(jnp.bfloat16)
    out_grad = lax.dot_general(
        attended, grad_out, contract_rows, preferred_element_type=jnp.float32
    ).astype(jnp.bfloat16)
    attended_grad = lax.dot_general(
        grad_out, out_weight, contract_cols, preferred_element_type=jnp.float32
    ).astype(jnp.bfloat16)
    query_grad, key_grad, value_grad, qkv_bias_local = attention_backward(
        bounds, start, cosine, sine, query, key, value, attended, attended_grad, log_sums
    )
    parts = (query_grad, key_grad, value_grad)
    term = lax.dot_general(
        act_grad_b, up_weight, contract_cols, preferred_element_type=jnp.float32
    )
    for index, part in enumerate(parts):
        term = term + lax.dot_general(
            part, qkv_weight[index], contract_cols, preferred_element_type=jnp.float32
        )
    hidden_grad = lax.psum_scatter(
        term.astype(jnp.bfloat16), "tensor", scatter_dimension=0, tiled=True
    ).astype(jnp.float32)
    qkv_grads = [
        lax.dot_general(hidden, part, contract_rows, preferred_element_type=jnp.float32).astype(
            jnp.bfloat16
        )
        for part in parts
    ]
    down_share = lax.psum_scatter(
        down_grad, "dp", scatter_dimension=1, tiled=True
    ).astype(jnp.float32)
    up_share = lax.psum_scatter(up_grad, "dp", scatter_dimension=0, tiled=True).astype(jnp.float32)
    out_share = lax.psum_scatter(
        out_grad, "dp", scatter_dimension=1, tiled=True
    ).astype(jnp.float32)
    qkv_share = lax.psum_scatter(
        jnp.stack(qkv_grads), "dp", scatter_dimension=1, tiled=True
    ).astype(jnp.float32)
    early = small_sum(lanes_of(qkv_bias_local, up_bias_local, bias_sum), (("dp", dp),), 1)
    qkv_rows, up_rows = 3 * cols // 128, units // 128
    qkv_bias_grad = early[:qkv_rows].reshape(3, cols)
    up_bias_grad = early[qkv_rows : qkv_rows + up_rows].reshape(units)
    bias_total = early[qkv_rows + up_rows :].reshape(depth)
    gain_local = jnp.sum(hidden_grad * normed, axis=0)
    shift_local = jnp.sum(hidden_grad, axis=0)
    late = small_sum(lanes_of(gain_local, shift_local), (("tensor", tensor), ("dp", dp)), 2)
    gain_grad, shift_grad = late.reshape(2, depth)
    scaled = hidden_grad * ln_gain
    inner = (
        scaled
        - jnp.mean(scaled, axis=-1, keepdims=True)
        - normed * jnp.mean(scaled * normed, axis=-1, keepdims=True)
    )
    input_grad = (cotangent.astype(jnp.float32) + inv_scale * inner).astype(jnp.bfloat16)
    return (
        block_out,
        input_grad,
        gain_grad,
        shift_grad,
        qkv_share,
        qkv_bias_grad,
        out_share,
        bias_total,
        up_share,
        up_bias_grad,
        down_share,
        bias_total,
    )


def solution(mesh):
    return jax.shard_map(
        functools.partial(local, (mesh.shape["dp"], mesh.shape["tensor"])),
        mesh=mesh,
        in_specs=(
            P(("dp", "tensor"), None),
            P(),
            P(),
            P(None, None, "tensor"),
            P(None, "tensor"),
            P("tensor", None),
            P(),
            P(None, "tensor"),
            P("tensor"),
            P("tensor", None),
            P(),
            P("dp"),
            P(("dp", "tensor"), None),
        ),
        out_specs=(
            P(("dp", "tensor"), None),
            P(("dp", "tensor"), None),
            P(),
            P(),
            P(None, "dp", "tensor"),
            P(None, "tensor"),
            P("tensor", "dp"),
            P(),
            P("dp", "tensor"),
            P("tensor"),
            P("tensor", "dp"),
            P(),
        ),
        check_vma=False,
    )
```

time: 1220 us -> 992 us (0.81)
  matrix products: 485 us -> 266 us
  Pallas kernels: 0 us -> 188 us
  waiting for transfers between devices: 557 us -> 460 us
  other arithmetic: 104 us -> 45.9 us
  local copies, waits for them, and re-layouts: 53.7 us -> 6.63 us
    dot_general x31 -> x10, matrix products: 364 us -> 141 us  [the longest x1 36.8 us: local(): lax.dot_general(act_grad_b, up_weight, contract_cols, preferred_element_t...]
    pallas_call x0 -> x5, Pallas kernels: none -> 188 us  [the longest x1 79.9 us: attention_backward(): pl.pallas_call(backward_kernel, out_shape=(shape, shape, shape, jax.Shape...]
    psum x1 -> x0, waiting for transfers between devices: 131 us -> none  [local(): lax.psum((qkv_bias_full, up_bias_full, bias_sum, gain_local, shift_local)...]
    all_gather x1, waiting for transfers between devices: 0.01 us -> 61.9 us  [local(): grad_out = lax.all_gather(cotangent, 'tensor', axis=0, tiled=True)]
    reduce_sum x6 -> x3, other arithmetic: 47.4 us -> 5.26 us  [the longest x1 4.84 us: local(): bias_sum = jnp.sum(grad_out.astype(jnp.float32), axis=0)]
    reduce_scatter x6, waiting for transfers between devices: 287 us -> 259 us  [the longest x1 131 us: local(): lax.psum_scatter(term.astype(jnp.bfloat16), 'tensor', scatter_dimension=0...]
    another operation x6 -> x2, local copies, waits for them, and re-layouts: 16.7 us -> 1.32 us  [the longest x1 1.32 us: local(): gain_grad, shift_grad = late.reshape(2, depth)]
    unnamed x139 -> x41, local copies, waits for them, and re-layouts: 16.4 us -> 1.93 us
  transfers between devices with their start and end apart: 9 -> 8, of which waited for: 5 -> 4; matrix products, arithmetic and copies ran while one was open for 38% -> 30% of each run, Pallas kernels for 0% -> 19%
where the time goes in v1:
time: 992 us; the launch traced here: 982 us
  waiting for transfers between devices  460 us (46%)
  matrix products  266 us (27%)
  Pallas kernels  188 us (19%)
  other arithmetic  45.9 us (5%)
  between operations  14.9 us (2%)
    all_gather x1, waiting for transfers between devices, local(): hidden = lax.all_gather(hidden_own, 'tensor', axis=0, tiled=True)  138 us
    reduce_scatter x1, waiting for transfers between devices, local(): lax.psum_scatter(term.astype(jnp.bfloat16), 'tensor', scatter_dimension=0...  131 us
    reduce_scatter x1, waiting for transfers between devices, local(): lax.psum_scatter((jnp.dot(attended, out_weight, preferred_element_type=jn...  129 us
    pallas_call x1, Pallas kernels, attention_backward(): pl.pallas_call(backward_kernel, out_shape=(shape, shape, shape, jax.Shape...  79.9 us
    pallas_call x1, Pallas kernels, attention_forward(): pl.pallas_call(forward_kernel, out_shape=(jax.ShapeDtypeStruct((length, c...  68.9 us
    all_gather x1, waiting for transfers between devices, local(): grad_out = lax.all_gather(cotangent, 'tensor', axis=0, tiled=True)  61.9 us
    dot_general x1, matrix products, local(): lax.dot_general(grad_out, down_weight, contract_cols, preferred_element_t...  36.9 us
    dot_general x1, matrix products, local(): lax.dot_general(act_grad_b, up_weight, contract_cols, preferred_element_t...  36.8 us
  transfers between devices with their start and end apart: 8, of which 4 were waited for; matrix products, arithmetic and copies ran while one was open for 30% of the time, Pallas kernels for 19%

profile of v1, /device:TPU:8, one launch (start us, length us, event | category | flops | bytes accessed | tf_op | source)
XLA Modules:
  0.0 982.1 jit_solution(11273805071754339541)
XLA Ops:
  7.2 2.1 convert_reduce_fusion.2
  9.3 2.3 fusion.21
  12.2 3.8 fusion.16
  16.1 0.7 all-gather.5.cloned.1.call-update
  17.1 0.6 fusion.47
  17.7 1.9 subtract_convert_fusion
  20.2 0.6 pad_add_fusion.bounds
  20.8 5.5 fusion.40
  26.3 137.7 %all-gather.3.cloned.1.call-done.hidden_ref = bf16[2048,2048]{1,0:T(8,128)(2,1)} async-done(((bf16[512,2048]{1,0:T(8,128)(2,1)}), bf16[2048,2048]{1,0:T(8,128)(2,1)}) %all-gather.3.cloned.1.call-update) | async-done | bytes 8388624 | tf_op jit(solution)/shard_map/all_gather | solution.py:441
  164.0 18.6 %project.1 = (bf16[2048,512]{1,0:T(8,128)(2,1)}, bf16[2048,512]{1,0:T(8,128)(2,1)}, bf16[2048,512]{1,0:T(8,128)(2,1)}) custom-call(bf16[2048,2048]{1,0:T(8,128)(2,1)} %all-gather.3.cloned.1.call-done.hidden_ref, bf16[3,2048,512]{2,1,0:T(8,128)(2,1)} %weight_ref.1, f32[3,512]{1,0:T(4,128)} %bias_ref.1, f32[2048,128]{1,0:T(8,128)} %get-tuple-element.48.cos_ref, ...), custom_call_target="tpu_custom_call" | custom-call | flops 12884901888 | bytes 20971520 | tf_op jit(solution)/shard_map/project/pallas_call | solution.py:385
  182.6 68.9 %attention_forward.1 = (bf16[2048,512]{1,0:T(8,128)(2,1)}, f32[4,2,2048]{2,1,0:T(2,128)}) custom-call(s32[4,8]{1,0:T(4,128)} %pad_add_fusion.bounds, s32[1,2048]{1,0:T(1,128)} %bitcast.79, bf16[2048,512]{1,0:T(8,128)(2,1)} %get-tuple-element.21.q_ref, bf16[2048,512]{1,0:T(8,128)(2,1)} %get-tuple-element.22.k_ref, bf16[2048,512]{1,0:T(8,128)(2,1)} %get-tuple-element.23.v_ref), custom_call_target="tpu_custom_call" | custom-call | flops 16000000000 | bytes 8388608 | tf_op jit(solution)/shard_map/attention_forward/pallas_call | solution.py:210
  251.4 61.9 %all-gather.5.cloned.1.call-done = bf16[2048,2048]{1,0:T(8,128)(2,1)} async-done(((bf16[512,2048]{1,0:T(8,128)(2,1)}), bf16[2048,2048]{1,0:T(8,128)(2,1)}) %all-gather.5.cloned.1.call-update) | async-done | bytes 8388624 | tf_op jit(solution)/shard_map/all_gather | solution.py:442
  313.4 9.9 %convolution_convert_fusion.2 = bf16[512,2048]{1,0:T(8,128)(2,1)} fusion(bf16[2048,512]{1,0:T(8,128)(2,1)} %get-tuple-element.24.out_ref, bf16[2048,2048]{1,0:T(8,128)(2,1)} %all-gather.5.cloned.1.call-done), kind=kOutput, calls=%fused_computation.43 | convolution fusion | flops 4296015872 | bytes 12582912 | tf_op jit(solution)/shard_map/dot_general | solution.py:473
  323.5 9.2 convolution_convert_fusion.6.grad_ref
  332.7 79.9 %attention_backward.1 = (bf16[2048,512]{1,0:T(8,128)(2,1)}, bf16[2048,512]{1,0:T(8,128)(2,1)}, bf16[2048,512]{1,0:T(8,128)(2,1)}, f32[3,512]{1,0:T(4,128)}) custom-call(s32[4,8]{1,0:T(4,128)} %pad_add_fusion.bounds, s32[1,2048]{1,0:T(1,128)} %bitcast.80, f32[2048,128]{1,0:T(8,128)} %get-tuple-element.48.cos_ref, f32[2048,128]{1,0:T(8,128)} %get-tuple-element.47.sin_ref, ...), custom_call_target="tpu_custom_call" | custom-call | flops 40000000000 | bytes 16777216 | tf_op jit(solution)/shard_map/attention_backward/pallas_call | solution.py:331
  412.7 8.7 fusion.27
  421.4 8.6 fusion.28
  430.1 4.8 fusion.29
  434.9 3.2 pad_maximum_fusion
  438.1 25.0 %fusion.49 = f32[2048,2048]{1,0:T(8,128)} fusion(bf16[2048,2048]{1,0:T(8,128)(2,1)} %all-gather.3.cloned.1.call-done.hidden_ref, bf16[2048,2048]{1,0:T(8,128)(2,1)} %param.20), kind=kOutput, calls=%fused_computation.108 | convolution fusion | flops 17179869184 | bytes 33554432 | tf_op jit(solution)/shard_map/dot_general | solution.py:447
  463.1 36.9 %fusion.6 = (f32[2048]{0:T(1024)}, bf16[2048,2048]{1,0:T(8,128)(2,1)}, f32[2048,2048]{1,0:T(8,128)}) fusion(f32[2048,2048]{1,0:T(8,128)} %fusion.49, f32[2048]{0:T(1024)S(1)} %copy-done.13, bf16[2048,2048]{1,0:T(8,128)(2,1)} %all-gather.5.cloned.1.call-done, bf16[2048,2048]{1,0:T(8,128)(2,1)} %param.22), kind=kOutput, calls=%fused_computation.13 | convolution fusion | flops 17272141824 | bytes 58736640 | tf_op jit(solution)/shard_map/dot_general | solution.py:465
  500.0 27.2 %convolution_convert_fusion.1 = bf16[2048,2048]{1,0:T(8,128)(2,1)} fusion(bf16[2048,2048]{1,0:T(8,128)(2,1)} %all-gather.3.cloned.1.call-done.hidden_ref, f32[2048,2048]{1,0:T(8,128)} %get-tuple-element.52, bf16[2048,2048]{1,0:T(8,128)(2,1)} %get-tuple-element.38), kind=kOutput, calls=%fused_computation.16 | convolution fusion | flops 17196646400 | bytes 41943040 | tf_op jit(solution)/shard_map/dot_general | solution.py:470
  527.3 27.3 %convolution_convert_fusion = bf16[2048,2048]{1,0:T(8,128)(2,1)} fusion(bf16[2048,2048]{1,0:T(8,128)(2,1)} %all-gather.5.cloned.1.call-done, f32[2048,2048]{1,0:T(8,128)} %fusion.49, f32[2048]{0:T(1024)S(1)} %copy-done.13), kind=kOutput, calls=%fused_computation.15 | convolution fusion | flops 17226006528 | bytes 33562624 | tf_op jit(solution)/shard_map/dot_general | solution.py:462
  554.6 13.1 %fusion.30 = f32[2048,2048]{1,0:T(8,128)} fusion(bf16[2048,512]{1,0:T(8,128)(2,1)} %get-tuple-element.28, bf16[3,2048,512]{2,1,0:T(8,128)(2,1)} %weight_ref.1), kind=kOutput, calls=%fused_computation.51 | convolution fusion | flops 4294967296 | bytes 20971520 | tf_op jit(solution)/shard_map/dot_general | solution.py:487
  567.7 9.9 %fusion.32 = f32[2048,2048]{1,0:T(8,128)} fusion(bf16[2048,512]{1,0:T(8,128)(2,1)S(1)} %copy-done.16, bf16[3,2048,512]{2,1,0:T(8,128)(2,1)} %weight_ref.1), kind=kOutput, calls=%fused_computation.53 | convolution fusion | flops 4294967296 | bytes 20971520 | tf_op jit(solution)/shard_map/dot_general | solution.py:487
  577.6 10.0 %fusion.34 = f32[2048,2048]{1,0:T(8,128)} fusion(bf16[2048,512]{1,0:T(8,128)(2,1)S(1)} %copy-done.14, bf16[3,2048,512]{2,1,0:T(8,128)(2,1)} %weight_ref.1), kind=kOutput, calls=%fused_computation.55 | convolution fusion | flops 4294967296 | bytes 20971520 | tf_op jit(solution)/shard_map/dot_general | solution.py:487
  587.7 36.8 %add_convert_fusion = bf16[2048,2048]{1,0:T(8,128)(2,1)} fusion(f32[2048,2048]{1,0:T(8,128)} %fusion.30, f32[2048,2048]{1,0:T(8,128)} %fusion.32, f32[2048,2048]{1,0:T(8,128)} %fusion.34, bf16[2048,2048]{1,0:T(8,128)(2,1)} %param.20, f32[2048,2048]{1,0:T(8,128)} %get-tuple-element.52, bf16[2048,2048]{1,0:T(8,128)(2,1)} %get-tuple-element.38), kind=kOutput, calls=%fused_computation.9 | convolution fusion | flops 17209229312 | bytes 92274688 | tf_op jit(solution)/shard_map/dot_general | solution.py:483
  624.5 10.3 %fusion.48 = f32[2048,2048]{1,0:T(8,128)} fusion(bf16[2048,512]{1,0:T(8,128)(2,1)} %get-tuple-element.24.out_ref, bf16[512,2048]{1,0:T(8,128)(2,1)S(1)} %copy-done), kind=kOutput, calls=%fused_computation.107 | convolution fusion | flops 4294967296 | bytes 20971520 | tf_op jit(solution)/shard_map/dot_general | solution.py:453
  634.8 28.6 %add_convert_fusion.1 = bf16[2048,2048]{1,0:T(8,128)(2,1)} fusion(f32[2048,2048]{1,0:T(8,128)} %fusion.48, bf16[2048,2048]{1,0:T(8,128)(2,1)} %param.22, f32[2048,2048]{1,0:T(8,128)} %fusion.49, f32[2048]{0:T(1024)S(1)} %copy-done.13), kind=kOutput, calls=%fused_computation.11 | convolution fusion | flops 17230200832 | bytes 50339840 | tf_op jit(solution)/shard_map/dot_general | solution.py:454
  663.4 0.7 copy-done.11
  664.1 4.8 convert_reduce_fusion
  668.9 0.6 pad_maximum_fusion.1.x_ref
  669.5 6.6 small_sum.3
  676.1 0.7 slice.43
  676.8 0.6 reshape.286
  677.4 1.4 slice_bitcast_fusion
  678.8 1.8 convert_element_type.112
  680.6 2.6 convert_element_type.109
  683.2 2.8 convert_element_type.114
  686.0 2.7 convert_element_type.116
  688.7 130.9 %reduce-scatter.9.cloned.1.call-done = bf16[512,2048]{1,0:T(8,128)(2,1)} async-done(((bf16[2048,2048]{1,0:T(8,128)(2,1)}), bf16[512,2048]{1,0:T(8,128)(2,1)}) %reduce-scatter.9.cloned.1.call-update) | async-done | bytes 2097168 | tf_op jit(solution)/shard_map/reduce_scatter | solution.py:490
  819.6 3.6 fusion.26
  823.2 0.6 pad_maximum_fusion.2.x_ref
  823.8 14.2 %small_sum.2 = f32[32,128]{1,0:T(8,128)} custom-call(f32[32,128]{1,0:T(8,128)} %pad_maximum_fusion.2.x_ref), custom_call_target="tpu_custom_call" | custom-call | tf_op jit(solution)/shard_map/small_sum/pallas_call | solution.py:87
  838.1 1.3 slice_bitcast_fusion.2
  839.4 128.6 %reduce-scatter.7.cloned.1.call-done = bf16[512,2048]{1,0:T(8,128)(2,1)} async-done(((bf16[2048,2048]{1,0:T(8,128)(2,1)}), bf16[512,2048]{1,0:T(8,128)(2,1)}) %reduce-scatter.7.cloned.1.call-update) | async-done | bytes 2097168 | tf_op jit(solution)/shard_map/reduce_scatter | solution.py:451
  968.0 6.3 fusion.20
  974.2 0.6 copy.26
  (78 shorter events, 2.1 us)
Async XLA Ops:
  7.2 316.4 %copy-start = (bf16[512,2048]{1,0:T(8,128)(2,1)S(1)}, bf16[512,2048]{1,0:T(8,128)(2,1)}, u32[]{:S(2)}) copy-start(bf16[512,2048]{1,0:T(8,128)(2,1)} %param.18) | copy-start | bytes 6291460
  7.2 9.7 copy-start.6
  7.2 156.8 %all-gather.3.cloned.1.call-start = ((), (), s32[]{:S(2)}) async-start(), calls=%async_computation.6 | async-start | bytes 10485760 | tf_op jit(solution)/shard_map/all_gather | solution.py:441
  9.3 2.3 copy-start.2
  11.6 0.6 copy-start.4
  16.0 297.4 %all-gather.5.cloned.1.call-start = ((), (), s32[]{:S(2)}) async-start(), calls=%async_computation.8 | async-start | bytes 10485760 | tf_op jit(solution)/shard_map/all_gather | solution.py:442
  16.8 662.0 %reduce-scatter.13.cloned.1.call-start = ((), (), s32[]{:S(2)}) async-start(), calls=%async_computation.11 | async-start | bytes 2359296 | tf_op jit(solution)/shard_map/reduce_scatter | solution.py:503
  19.7 162.9 %copy-start.7 = (s32[2048]{0:T(1024)}, s32[2048]{0:T(1024)S(1)}, u32[]{:S(2)}) copy-start(s32[2048]{0:T(1024)S(1)} %get-tuple-element.40) | copy-start | bytes 24580
  323.3 357.3 %reduce-scatter.11.cloned.1.call-start = ((), (), s32[]{:S(2)}) async-start(), calls=%async_computation.10 | async-start | bytes 7077888 | tf_op jit(solution)/shard_map/reduce_scatter | solution.py:506
  412.7 8.7 copy-start.15
  412.7 17.4 %slice-start = ((s8[8388608]{0:T(1024)(128)(4,1)}), s8[4194304]{0:T(1024)(128)(4,1)S(1)}, s32[]{:S(2)}) async-start(s8[8388608]{0:T(1024)(128)(4,1)} %bitcast.82), calls=%async_computation.14 | async-start | bytes 8388608
  421.4 8.7 slice-start.1
  421.4 8.6 copy-start.17
  438.0 25.1 %copy-start.13 = (f32[2048]{0:T(1024)S(1)}, f32[2048]{0:T(1024)}, u32[]{:S(2)}) copy-start(f32[2048]{0:T(1024)} %param.21) | copy-start | bytes 24580
  438.1 245.1 %reduce-scatter.15.cloned.1.call-start = ((), (), s32[]{:S(2)}) async-start(), calls=%async_computation.12 | async-start | bytes 9437184 | tf_op jit(solution)/shard_map/reduce_scatter | solution.py:502
  527.2 158.8 %reduce-scatter.17.cloned.1.call-start = ((), (), s32[]{:S(2)}) async-start(), calls=%async_computation.13 | async-start | bytes 9437184 | tf_op jit(solution)/shard_map/reduce_scatter | solution.py:499
  554.6 265.0 %reduce-scatter.9.cloned.1.call-start = ((), (), s32[]{:S(2)}) async-start(), calls=%async_computation.9 | async-start | bytes 10485760 | tf_op jit(solution)/shard_map/reduce_scatter | solution.py:490
  554.6 13.1 %copy-start.16 = (bf16[2048,512]{1,0:T(8,128)(2,1)S(1)}, bf16[2048,512]{1,0:T(8,128)(2,1)}, u32[]{:S(2)}) copy-start(bf16[2048,512]{1,0:T(8,128)(2,1)} %get-tuple-element.27) | copy-start | bytes 6291460
  567.7 9.9 %copy-start.14 = (bf16[2048,512]{1,0:T(8,128)(2,1)S(1)}, bf16[2048,512]{1,0:T(8,128)(2,1)}, u32[]{:S(2)}) copy-start(bf16[2048,512]{1,0:T(8,128)(2,1)} %get-tuple-element.26) | copy-start | bytes 6291460
  624.4 343.5 %reduce-scatter.7.cloned.1.call-start = ((), (), s32[]{:S(2)}) async-start(), calls=%async_computation.7 | async-start | bytes 10485760 | tf_op jit(solution)/shard_map/reduce_scatter | solution.py:451
  663.3 0.7 copy-start.11
  663.3 5.6 copy-start.12
  664.0 155.5 %copy-start.1 = (f32[2048]{0:T(1024)S(1)}, f32[2048]{0:T(1024)}, u32[]{:S(2)}) copy-start(f32[2048]{0:T(1024)} %param.14) | copy-start | bytes 24580
  664.0 155.5 %copy-start.3 = (f32[512]{0:T(512)S(1)}, f32[512]{0:T(512)}, u32[]{:S(2)}) copy-start(f32[512]{0:T(512)} %copy-done.2) | copy-start | bytes 6148
  664.0 155.5 %copy-start.5 = (f32[512]{0:T(512)S(1)}, f32[512]{0:T(512)}, u32[]{:S(2)}) copy-start(f32[512]{0:T(512)} %copy-done.4) | copy-start | bytes 6148
  668.9 299.1 %copy-start.9 = (f32[2048]{0:T(1024)S(1)}, f32[2048]{0:T(1024)}, u32[]{:S(2)}) copy-start(f32[2048]{0:T(1024)} %param.23) | copy-start | bytes 24580
  668.9 299.0 %copy-start.10 = (f32[2048]{0:T(1024)S(1)}, f32[2048]{0:T(1024)}, u32[]{:S(2)}) copy-start(f32[2048]{0:T(1024)} %param.19) | copy-start | bytes 24580
  678.8 295.4 %copy-start.8 = (f32[2048]{0:T(1024)}, f32[2048]{0:T(1024)S(1)}, u32[]{:S(2)}) copy-start(f32[2048]{0:T(1024)S(1)} %get-tuple-element.80) | copy-start | bytes 24580
Sparse Core Ops, SparseCore 0:
  16.1 147.8 all-gather.2
  165.6 147.7 all-gather.4
  323.4 42.3 reduce-scatter.12
  438.2 60.9 reduce-scatter.10
  527.3 70.9 reduce-scatter.14
  601.6 71.2 reduce-scatter.16
  675.3 144.1 reduce-scatter.8
  821.9 146.0 reduce-scatter.6
